TPU v7x, 32 devices: a whole 2x2x4 slice. The times are simulated.
32 devices in a mesh: group: 4 (over x, core), seq: 2 (over y), expert: 4 (over z).
Axes of the slice: x: 2, y: 2, z: 4, core: 2. Of those that a mesh axis runs over, the one named last changes fastest.
Arguments:
- queries: bfloat16 [16, 32, 128], P('expert', 'group')
- keys: bfloat16 [16, 256, 8, 128], P('expert', 'seq', 'group')
- values: bfloat16 [16, 256, 8, 128], P('expert', 'seq', 'group'), may hold values from -48 to 48
- block_of_slot: int32 [16, 16], P('expert', 'seq'), may hold values from 0 to 15, each once within a row
- lengths: int32 [16], P('expert'), may hold values from 128 to 256
- out_proj: bfloat16 [4096, 4096], P('group', 'seq'), may hold values from -0.09375 to 0.09375
- residual: bfloat16 [16, 4096], P('expert', 'seq'), may hold values from -6 to 6
- norm_gain: bfloat16 [4096], replicated, may hold values from 0.25 to 1.75
- router: bfloat16 [4096, 8], replicated, may hold values from -0.09375 to 0.09375
- routes: int32 [16, 2], P('expert'), may hold values from 0 to 7, all different within a row; in each aligned block of 4 rows (0 to 3, 4 to 7, ...) at most 2 rows name the same one
- w_gate: bfloat16 [8, 4096, 14336], P('expert', None, ('group', 'seq')), may hold values from -0.09375 to 0.09375
- w_up: bfloat16 [8, 4096, 14336], P('expert', None, ('group', 'seq')), may hold values from -0.09375 to 0.09375
- w_down: bfloat16 [8, 14336, 4096], P('expert', ('group', 'seq')), may hold values from -0.046875 to 0.046875
Outputs:
- layer_out: bfloat16 [16, 4096], P('expert', 'seq')
Inputs may be any that keep to these rules, and one draw needn't show every extreme that they name: `block_of_slot`: each row lists every logical block once. `routes`: the two ids of a row differ; among the 4 rows of one device no expert is named more than 2 times, and in some such blocks one expert is named exactly 2 times.
All inputs are finite; a program needn't handle non-finite values.
Results may differ from a plain program's by a relative error of at most 0.013.
Values may be sent and summed in bfloat16 or wider, within the bound.
No kernel may reach another device: no remote copies, remote signals or barrier semaphores. Data moves between devices by JAX's collectives and lax.ppermute only.
A program may use at most 128 MiB of HBM per device.

v0:
```python
import jax
import jax.numpy as jnp
from jax import lax
from jax.sharding import PartitionSpec as P

BLOCK = 16
CAPACITY = 2
masked_score = -1e30


def combined_all(value, axis, combine):
    everything = jax.tree.map(lambda part: lax.all_gather(part, axis), value)
    initial = jax.tree.map(lambda part: part[0], everything)

    def hop(k, so_far):
        return combine(so_far, jax.tree.map(lambda part: part[k], everything))

    return lax.fori_loop(1, lax.axis_size(axis), hop, initial)


def combine_carry(earlier, later):
    high_a, total_a, sums_a = earlier
    high_b, total_b, sums_b = later
    highest = jnp.maximum(high_a, high_b)
    scale_a = jnp.exp(high_a - highest)
    scale_b = jnp.exp(high_b - highest)
    return (
        highest,
        total_a * scale_a + total_b * scale_b,
        sums_a * scale_a[..., None] + sums_b * scale_b[..., None],
    )


def shards(
    queries,
    keys,
    values,
    block_of_slot,
    lengths,
    out_proj,
    residual,
    norm_gain,
    router,
    routes,
    w_gate,
    w_up,
    w_down,
):
    batch_rows, local_heads, head_dim = queries.shape
    span_len = keys.shape[1]
    kv_local = keys.shape[2]
    per_kv = local_heads // kv_local
    grouped = queries.reshape(batch_rows, kv_local, per_kv, head_dim)
    scores = jnp.einsum(
        "rkgd,rlkd->rkgl", grouped, keys, preferred_element_type=jnp.float32
    ) * head_dim ** (-0.5)
    offsets = jnp.arange(BLOCK, dtype=jnp.int32)
    position = (block_of_slot[:, :, None] * BLOCK + offsets[None, None, :]).reshape(
        batch_rows, span_len
    )
    visible = (position < lengths[:, None])[:, None, None, :]
    masked = jnp.where(visible, scores, masked_score)
    highest = jnp.max(masked, axis=-1)
    probs = jnp.where(visible, jnp.exp(masked - highest[..., None]), 0.0)
    totals = jnp.sum(probs, axis=-1)
    weighted = jnp.einsum(
        "rkgl,rlkd->rkgd", probs.astype(jnp.bfloat16), values, preferred_element_type=jnp.float32
    )
    local_carry = (highest, totals, weighted)
    highest, totals, weighted = combined_all(local_carry, "seq", combine_carry)
    attended = (
        (weighted / totals[..., None])
        .astype(jnp.bfloat16)
        .reshape(batch_rows, local_heads * head_dim)
    )
    partial_value = jnp.dot(attended, out_proj, preferred_element_type=jnp.float32)
    attention = lax.psum(partial_value, "group")
    hidden = residual.astype(jnp.float32) + attention
    full_rows = lax.all_gather(hidden, "seq", axis=1, tiled=True)
    meansq = jnp.mean(full_rows * full_rows, axis=-1, keepdims=True)
    normed = (full_rows * lax.rsqrt(meansq + 1e-05) * norm_gain.astype(jnp.float32)).astype(
        jnp.bfloat16
    )
    logits = jnp.dot(normed, router, preferred_element_type=jnp.float32)
    experts = router.shape[1]
    onehot = (routes[:, :, None] == jnp.arange(experts, dtype=jnp.int32)[None, None, :]).astype(
        jnp.int32
    )
    chosen = jnp.sum(onehot.astype(jnp.float32) * logits[:, None, :], axis=-1)
    gate_probs = jax.nn.softmax(chosen, axis=-1)
    per_row = jnp.sum(onehot, axis=1)
    earlier = jnp.cumsum(per_row, axis=0) - per_row
    slot_index = jnp.sum(onehot * earlier[:, None, :], axis=2)
    in_slot = (
        slot_index[:, :, None] == jnp.arange(CAPACITY, dtype=jnp.int32)[None, None, :]
    ).astype(jnp.int32)
    chart = onehot[:, :, :, None] * in_slot[:, :, None, :]
    picker = jnp.sum(chart, axis=1).astype(jnp.bfloat16)
    outbound = jnp.einsum("rec,rd->ecd", picker, normed, preferred_element_type=jnp.float32).astype(
        jnp.bfloat16
    )
    expert_devs = lax.axis_size("expert")
    local_experts = experts // expert_devs
    model_width = normed.shape[1]
    outbound = outbound.reshape(expert_devs, local_experts, CAPACITY, model_width)
    inbound = lax.all_to_all(outbound, "expert", split_axis=0, concat_axis=0, tiled=True)
    gate_act = jnp.einsum("secd,edf->secf", inbound, w_gate, preferred_element_type=jnp.float32)
    upper = jnp.einsum("secd,edf->secf", inbound, w_up, preferred_element_type=jnp.float32)
    activated = (jax.nn.silu(gate_act) * upper).astype(jnp.bfloat16)
    down_terms = jnp.einsum("secf,efd->secd", activated, w_down, preferred_element_type=jnp.float32)
    summed = lax.psum(down_terms.astype(jnp.bfloat16), ("group", "seq")).astype(jnp.float32)
    col_width = summed.shape[3] // lax.axis_size("seq")
    my_cols = lax.dynamic_slice_in_dim(summed, lax.axis_index("seq") * col_width, col_width, 3)
    returned = lax.all_to_all(
        my_cols.astype(jnp.bfloat16), "expert", split_axis=0, concat_axis=0, tiled=True
    )
    returned = returned.reshape(experts, CAPACITY, returned.shape[3]).astype(jnp.float32)
    mixing = jnp.sum(gate_probs[:, :, None, None] * chart.astype(jnp.float32), axis=1)
    expert_mix = jnp.einsum("rec,ecd->rd", mixing, returned, precision=lax.Precision.HIGHEST)
    return (hidden + expert_mix).astype(jnp.bfloat16)


def solution(mesh):
    return jax.shard_map(
        shards,
        mesh=mesh,
        in_specs=(
            P("expert", "group", None),
            P("expert", "seq", "group", None),
            P("expert", "seq", "group", None),
            P("expert", "seq"),
            P("expert"),
            P("group", "seq"),
            P("expert", "seq"),
            P(),
            P(),
            P("expert", None),
            P("expert", None, ("group", "seq")),
            P("expert", None, ("group", "seq")),
            P("expert", ("group", "seq"), None),
        ),
        out_specs=P("expert", "seq"),
        check_vma=False,
    )
```

profile of v0, /device:TPU:0, one launch (start us, length us, event | category | flops | bytes accessed | tf_op | source)
XLA Modules:
  0.0 164.8 jit_solution(3506737250032493510)
XLA Ops:
  6.5 0.0 copy-start
  6.5 0.8 fusion.56
  7.3 0.7 fusion.55
  8.1 0.7 broadcast_multiply_fusion
  8.8 0.1 add.70
  8.8 0.1 add.71
  8.9 0.1 add.73
  9.0 0.7 add_compare_fusion
  9.8 0.0 copy-done
  9.8 1.0 fusion.64
  10.8 5.3 %all-gather.1 = f32[8,2,4]{2,1,0:T(2,128)S(1)} all-gather(f32[4,2,4]{2,1,0:T(2,128)S(1)} %get-tuple-element.22), channel_id=3, replica_groups=mesh['group'=4,'seq'=2,'expert'=4] {'seq'}, dimensions={0}, use_global_device_ids=true | all-gather | bytes 384 | tf_op jit(solution)/shard_map/all_gather | solution.py:12
  16.1 0.2 fusion.44
  16.3 1.2 fusion.29
  17.4 4.4 %all-gather = f32[8,2,4,128]{3,2,1,0:T(4,128)S(1)} all-gather(f32[4,2,4,128]{3,2,1,0:T(4,128)S(1)} %fusion.29), channel_id=2, replica_groups=mesh['group'=4,'seq'=2,'expert'=4] {'seq'}, dimensions={0}, use_global_device_ids=true | all-gather | bytes 49152 | tf_op jit(solution)/shard_map/all_gather | solution.py:12
  21.8 4.3 %all-gather.2 = f32[8,2,4]{2,1,0:T(2,128)S(1)} all-gather(f32[4,2,4]{2,1,0:T(2,128)S(1)} %fusion.44), channel_id=4, replica_groups=mesh['group'=4,'seq'=2,'expert'=4] {'seq'}, dimensions={0}, use_global_device_ids=true | all-gather | bytes 384 | tf_op jit(solution)/shard_map/all_gather | solution.py:12
  26.2 0.1 fusion.43
  26.3 2.8 %fusion.65 = f32[4,2048]{1,0:T(4,128)S(1)} fusion(bf16[4,1024]{1,0:T(4,128)(2,1)S(1)} %reshape.183, bf16[1024,2048]{1,0:T(8,128)(2,1)} %param.18), kind=kOutput, calls=%fused_computation.72 | convolution fusion | flops 16777216 | bytes 4235264 | tf_op jit(solution)/shard_map/dot_general | solution.py:76
  29.2 10.3 %psum.14 = f32[4,2048]{1,0:T(4,128)S(1)} all-reduce(f32[4,2048]{1,0:T(4,128)S(1)} %fusion.65), channel_id=1, replica_groups=mesh['group'=4,'seq'=2,'expert'=4] {'group'}, use_global_device_ids=true, to_apply=%region_2.3 | all-reduce | flops 8192 | bytes 65536 | tf_op jit(solution)/shard_map/psum | solution.py:77
  39.5 0.9 select_reduce_fusion
  40.4 0.7 convert_add_fusion
  41.1 4.6 %all_gather.27 = f32[4,4096]{1,0:T(4,128)S(1)} all-gather(f32[4,2048]{1,0:T(4,128)S(1)} %convert_add_fusion), channel_id=1, replica_groups=mesh['group'=4,'seq'=2,'expert'=4] {'seq'}, dimensions={1}, use_global_device_ids=true | all-gather | bytes 98304 | tf_op jit(solution)/shard_map/all_gather | solution.py:79
  45.7 0.7 convert_element_type.66
  46.4 0.1 multiply_reduce_fusion
  46.6 0.1 multiply_convert_fusion
  46.7 0.1 multiply_reduce_fusion.1
  46.7 0.2 convolution_convert_fusion
  47.0 0.8 copy.42
  47.7 5.4 %all-to-all-start = ((bf16[4,2,2,4096]{3,2,1,0:T(2,128)(2,1)}), bf16[4,2,2,4096]{3,2,1,0:T(2,128)(2,1)S(1)}, u32[]{:S(2)}, u32[]{:S(2)}) async-start(bf16[4,2,2,4096]{3,2,1,0:T(2,128)(2,1)} %bitcast.2), calls=%async_computation | async-start | bytes 262144 | tf_op jit(solution)/shard_map/all_to_all | solution.py:106
  53.1 0.0 all-reduce.2.cloned.1.call-start
  53.1 1.0 fusion.66
  54.1 0.9 multiply_reduce_fusion.2
  55.0 4.0 %all-to-all-done = bf16[4,2,2,4096]{3,2,1,0:T(2,128)(2,1)S(1)} async-done(((bf16[4,2,2,4096]{3,2,1,0:T(2,128)(2,1)}), bf16[4,2,2,4096]{3,2,1,0:T(2,128)(2,1)S(1)}, u32[]{:S(2)}, u32[]{:S(2)}) %all-to-all-start) | async-done | bytes 131104 | tf_op jit(solution)/shard_map/all_to_all | solution.py:106
  59.1 11.6 %fusion.12 = f32[4,2,2,1792]{3,0,2,1:T(4,128)S(1)} fusion(bf16[2,4096,1792]{2,1,0:T(8,128)(2,1)} %param.23, bf16[4,2,2,4096]{3,2,1,0:T(2,128)(2,1)S(1)} %all-to-all-done), kind=kOutput, calls=%fused_computation.9 | convolution fusion | flops 234881024 | bytes 29605888 | tf_op jit(solution)/shard_map/secd,edf->secf/dot_general | solution.py:107
  70.6 21.8 %fusion.9 = bf16[4,2,2,4096]{3,0,2,1:T(4,128)(2,1)} fusion(bf16[2,1792,4096]{2,1,0:T(8,128)(2,1)} %param.25, bf16[2,4096,1792]{2,1,0:T(8,128)(2,1)} %param.24, f32[4,2,2,1792]{3,0,2,1:T(4,128)S(1)} %fusion.12, bf16[4,2,2,4096]{3,2,1,0:T(2,128)(2,1)S(1)} %all-to-all-done), kind=kOutput, calls=%fused_computation.8 | convolution fusion | flops 469999616 | bytes 59097088 | tf_op jit(solution)/shard_map/secf,efd->secd/dot_general | solution.py:110
  92.4 0.0 all-reduce.2.cloned.1.call-update
  92.5 52.7 %all-reduce.2.cloned.1.call-done = bf16[4,2,2,4096]{3,0,2,1:T(4,128)(2,1)} async-done(((bf16[4,2,2,4096]{3,0,2,1:T(4,128)(2,1)}), bf16[4,2,2,4096]{3,0,2,1:T(4,128)(2,1)}) %all-reduce.2.cloned.1.call-update) | async-done | bytes 131088 | tf_op jit(solution)/shard_map/psum | solution.py:111
  145.2 0.9 convert_convert_fusion
  146.1 0.7 copy.37
  146.8 4.6 %all-to-all-start.1 = ((bf16[4,2,2,2048]{3,2,1,0:T(2,128)(2,1)}), bf16[4,2,2,2048]{3,2,1,0:T(2,128)(2,1)S(1)}, u32[]{:S(2)}, u32[]{:S(2)}) async-start(bf16[4,2,2,2048]{3,2,1,0:T(2,128)(2,1)} %copy.37), calls=%async_computation.1 | async-start | bytes 131072 | tf_op jit(solution)/shard_map/all_to_all | solution.py:114
  151.4 0.1 fusion.48
  151.5 5.7 %all-to-all-done.1 = bf16[4,2,2,2048]{3,2,1,0:T(2,128)(2,1)S(1)} async-done(((bf16[4,2,2,2048]{3,2,1,0:T(2,128)(2,1)}), bf16[4,2,2,2048]{3,2,1,0:T(2,128)(2,1)S(1)}, u32[]{:S(2)}, u32[]{:S(2)}) %all-to-all-start.1) | async-done | bytes 65568 | tf_op jit(solution)/shard_map/all_to_all | solution.py:114
  157.1 0.8 fusion.27
  (10 shorter events, 0.1 us)
Async XLA Ops:
  6.5 3.2 %copy-start = (bf16[4,128,2,128]{3,2,1,0:T(2,128)(2,1)S(1)}, bf16[4,128,2,128]{3,2,1,0:T(2,128)(2,1)}, u32[]{:S(2)}) copy-start(bf16[4,128,2,128]{3,2,1,0:T(2,128)(2,1)} %param.14) | copy-start | bytes 786436
  47.7 11.3 %all-to-all-start = ((bf16[4,2,2,4096]{3,2,1,0:T(2,128)(2,1)}), bf16[4,2,2,4096]{3,2,1,0:T(2,128)(2,1)S(1)}, u32[]{:S(2)}, u32[]{:S(2)}) async-start(bf16[4,2,2,4096]{3,2,1,0:T(2,128)(2,1)} %bitcast.2), calls=%async_computation | async-start | bytes 262144 | tf_op jit(solution)/shard_map/all_to_all | solution.py:106
  53.1 92.1 %all-reduce.2.cloned.1.call-start = ((), (), s32[]{:S(2)}) async-start(), calls=%async_computation.2 | async-start | bytes 262144 | tf_op jit(solution)/shard_map/psum | solution.py:111
  146.8 10.3 %all-to-all-start.1 = ((bf16[4,2,2,2048]{3,2,1,0:T(2,128)(2,1)}), bf16[4,2,2,2048]{3,2,1,0:T(2,128)(2,1)S(1)}, u32[]{:S(2)}, u32[]{:S(2)}) async-start(bf16[4,2,2,2048]{3,2,1,0:T(2,128)(2,1)} %copy.37), calls=%async_computation.1 | async-start | bytes 131072 | tf_op jit(solution)/shard_map/all_to_all | solution.py:114
Sparse Core Ops, SparseCore 0:
  92.6 52.6 all-reduce.1
where the time goes:
time: 166 us; the launch traced here: 165 us
  waiting for transfers between devices  62.5 us (38%)
  matrix products  40.5 us (24%)
  blocking collectives  28.9 us (17%)
  between operations  13.5 us (8%)
  starting transfers between devices  9.99 us (6%)
  other arithmetic  7.8 us (5%)
  local copies, waits for them, and re-layouts  1.72 us (1%)
    psum x1, waiting for transfers between devices, shards(): lax.psum(down_terms.astype(jnp.bfloat16), ('group', 'seq'))  52.7 us
    dot_general x1, matrix products, shards(): jnp.einsum('secf,efd->secd', activated, w_down, preferred_element_type=jn...  21.8 us
    all_gather x3, blocking collectives, combined_all(): everything = jax.tree.map(lambda part: lax.all_gather(part, axis), value)  14.1 us
    dot_general x1, matrix products, shards(): jnp.einsum('secd,edf->secf', inbound, w_gate, preferred_element_type=jnp....  11.6 us
    psum x1, blocking collectives, shards(): attention = lax.psum(partial_value, 'group')  10.3 us
    all_to_all x1, waiting for transfers between devices, shards(): lax.all_to_all(my_cols.astype(jnp.bfloat16), 'expert', split_axis=0, conc...  5.66 us
    all_to_all x1, starting transfers between devices, shards(): lax.all_to_all(outbound, 'expert', split_axis=0, concat_axis=0, tiled=True)  5.39 us
    all_to_all x1, starting transfers between devices, shards(): lax.all_to_all(my_cols.astype(jnp.bfloat16), 'expert', split_axis=0, conc...  4.59 us
  transfers between devices with their start and end apart: 3, of which 3 were waited for; matrix products, arithmetic and copies ran while one was open for 1% of the time, Pallas kernels for 0%

commit v1 on v0

--- a/solution.py
+++ b/solution.py
@@ -6,6 +6,12 @@
 BLOCK = 16
 CAPACITY = 2
 masked_score = -1e30
+
+
+def summed_here(x, name):
+    blocks = lax.all_gather(x, name, axis=0, tiled=False)
+    acc = blocks.sum(axis=0)
+    return acc
 
 
 def combined_all(value, axis, combine):
@@ -74,7 +80,7 @@
         .reshape(batch_rows, local_heads * head_dim)
     )
     partial_value = jnp.dot(attended, out_proj, preferred_element_type=jnp.float32)
-    attention = lax.psum(partial_value, "group")
+    attention = summed_here(partial_value, "group")
     hidden = residual.astype(jnp.float32) + attention
     full_rows = lax.all_gather(hidden, "seq", axis=1, tiled=True)
     meansq = jnp.mean(full_rows * full_rows, axis=-1, keepdims=True)

time: 166 us -> 161 us (0.970)
  blocking collectives: 28.9 us -> 24.2 us
    psum x1 -> x0, blocking collectives: 10.3 us -> none  [shards(): attention = lax.psum(partial_value, 'group')]
    all_gather x0 -> x1, blocking collectives: none -> 5.54 us  [summed_here(): blocks = lax.all_gather(x, name, axis=0, tiled=False)]
where the time goes in v1:
time: 161 us; the launch traced here: 160 us
  waiting for transfers between devices  62.3 us (39%)
  matrix products  40.5 us (25%)
  blocking collectives  24.2 us (15%)
  between operations  13.5 us (8%)
  starting transfers between devices  9.85 us (6%)
  other arithmetic  7.82 us (5%)
  local copies, waits for them, and re-layouts  1.72 us (1%)
    psum x1, waiting for transfers between devices, shards(): lax.psum(down_terms.astype(jnp.bfloat16), ('group', 'seq'))  52.6 us
    dot_general x1, matrix products, shards(): jnp.einsum('secf,efd->secd', activated, w_down, preferred_element_type=jn...  21.8 us
    all_gather x3, blocking collectives, combined_all(): everything = jax.tree.map(lambda part: lax.all_gather(part, axis), value)  14.1 us
    dot_general x1, matrix products, shards(): jnp.einsum('secd,edf->secf', inbound, w_gate, preferred_element_type=jnp....  11.6 us
    all_to_all x1, waiting for transfers between devices, shards(): lax.all_to_all(my_cols.astype(jnp.bfloat16), 'expert', split_axis=0, conc...  5.66 us
    all_gather x1, blocking collectives, summed_here(): blocks = lax.all_gather(x, name, axis=0, tiled=False)  5.54 us
    all_to_all x1, starting transfers between devices, shards(): lax.all_to_all(outbound, 'expert', split_axis=0, concat_axis=0, tiled=True)  5.25 us
    all_to_all x1, starting transfers between devices, shards(): lax.all_to_all(my_cols.astype(jnp.bfloat16), 'expert', split_axis=0, conc...  4.59 us
  transfers between devices with their start and end apart: 3, of which 3 were waited for; matrix products, arithmetic and copies ran while one was open for 1% of the time, Pallas kernels for 0%

profile of v1, /device:TPU:0, one launch (start us, length us, event | category | flops | bytes accessed | tf_op | source)
XLA Modules:
  0.0 159.9 jit_solution(5313841566095392656)
XLA Ops:
  6.5 0.0 copy-start
  6.5 0.8 fusion.56
  7.3 0.7 fusion.55
  8.1 0.7 broadcast_multiply_fusion
  8.8 0.1 add.68
  8.8 0.1 add.69
  8.9 0.1 add.71
  9.0 0.7 add_compare_fusion
  9.8 0.0 copy-done
  9.8 1.0 fusion.64
  10.8 5.3 %all-gather.1 = f32[8,2,4]{2,1,0:T(2,128)S(1)} all-gather(f32[4,2,4]{2,1,0:T(2,128)S(1)} %get-tuple-element.22), channel_id=3, replica_groups=mesh['group'=4,'seq'=2,'expert'=4] {'seq'}, dimensions={0}, use_global_device_ids=true | all-gather | bytes 384 | tf_op jit(solution)/shard_map/all_gather | solution.py:18
  16.1 0.2 fusion.44
  16.3 1.2 fusion.29
  17.4 4.4 %all-gather = f32[8,2,4,128]{3,2,1,0:T(4,128)S(1)} all-gather(f32[4,2,4,128]{3,2,1,0:T(4,128)S(1)} %fusion.29), channel_id=2, replica_groups=mesh['group'=4,'seq'=2,'expert'=4] {'seq'}, dimensions={0}, use_global_device_ids=true | all-gather | bytes 49152 | tf_op jit(solution)/shard_map/all_gather | solution.py:18
  21.8 4.3 %all-gather.2 = f32[8,2,4]{2,1,0:T(2,128)S(1)} all-gather(f32[4,2,4]{2,1,0:T(2,128)S(1)} %fusion.44), channel_id=4, replica_groups=mesh['group'=4,'seq'=2,'expert'=4] {'seq'}, dimensions={0}, use_global_device_ids=true | all-gather | bytes 384 | tf_op jit(solution)/shard_map/all_gather | solution.py:18
  26.2 0.1 fusion.43
  26.3 2.8 %convolution_bitcast_fusion.1 = f32[1,4,2048]{2,1,0:T(4,128)S(1)} fusion(bf16[4,1024]{1,0:T(4,128)(2,1)S(1)} %reshape.186, bf16[1024,2048]{1,0:T(8,128)(2,1)} %param.18), kind=kOutput, calls=%fused_computation.12 | convolution fusion | flops 16777216 | bytes 4235264 | tf_op jit(solution)/shard_map/dot_general | solution.py:82
  29.2 5.5 %all-gather.4 = f32[4,4,2048]{2,1,0:T(4,128)S(1)} all-gather(f32[1,4,2048]{2,1,0:T(4,128)S(1)} %convolution_bitcast_fusion.1), channel_id=5, replica_groups=mesh['group'=4,'seq'=2,'expert'=4] {'group'}, dimensions={0}, use_global_device_ids=true | all-gather | bytes 163840 | tf_op jit(solution)/shard_map/all_gather | solution.py:12
  34.8 0.9 select_reduce_fusion
  35.7 0.7 convert_add_fusion
  36.4 4.6 %all_gather.35 = f32[4,4096]{1,0:T(4,128)S(1)} all-gather(f32[4,2048]{1,0:T(4,128)S(1)} %convert_add_fusion), channel_id=1, replica_groups=mesh['group'=4,'seq'=2,'expert'=4] {'seq'}, dimensions={1}, use_global_device_ids=true | all-gather | bytes 98304 | tf_op jit(solution)/shard_map/all_gather | solution.py:85
  41.0 0.7 convert_element_type.66
  41.7 0.1 multiply_reduce_fusion
  41.9 0.1 multiply_convert_fusion
  42.0 0.1 multiply_reduce_fusion.1
  42.0 0.2 convolution_convert_fusion
  42.3 0.8 copy.42
  43.1 5.3 %all-to-all-start = ((bf16[4,2,2,4096]{3,2,1,0:T(2,128)(2,1)}), bf16[4,2,2,4096]{3,2,1,0:T(2,128)(2,1)S(1)}, u32[]{:S(2)}, u32[]{:S(2)}) async-start(bf16[4,2,2,4096]{3,2,1,0:T(2,128)(2,1)} %bitcast.3), calls=%async_computation | async-start | bytes 262144 | tf_op jit(solution)/shard_map/all_to_all | solution.py:112
  48.3 0.0 all-reduce.2.cloned.1.call-start
  48.3 1.0 fusion.65
  49.3 0.9 multiply_reduce_fusion.2
  50.2 4.0 %all-to-all-done = bf16[4,2,2,4096]{3,2,1,0:T(2,128)(2,1)S(1)} async-done(((bf16[4,2,2,4096]{3,2,1,0:T(2,128)(2,1)}), bf16[4,2,2,4096]{3,2,1,0:T(2,128)(2,1)S(1)}, u32[]{:S(2)}, u32[]{:S(2)}) %all-to-all-start) | async-done | bytes 131104 | tf_op jit(solution)/shard_map/all_to_all | solution.py:112
  54.2 11.6 %fusion.12 = f32[4,2,2,1792]{3,0,2,1:T(4,128)S(1)} fusion(bf16[2,4096,1792]{2,1,0:T(8,128)(2,1)} %param.23, bf16[4,2,2,4096]{3,2,1,0:T(2,128)(2,1)S(1)} %all-to-all-done), kind=kOutput, calls=%fused_computation.9 | convolution fusion | flops 234881024 | bytes 29605888 | tf_op jit(solution)/shard_map/secd,edf->secf/dot_general | solution.py:113
  65.8 21.8 %fusion.9 = bf16[4,2,2,4096]{3,0,2,1:T(4,128)(2,1)} fusion(bf16[2,1792,4096]{2,1,0:T(8,128)(2,1)} %param.25, bf16[2,4096,1792]{2,1,0:T(8,128)(2,1)} %param.24, f32[4,2,2,1792]{3,0,2,1:T(4,128)S(1)} %fusion.12, bf16[4,2,2,4096]{3,2,1,0:T(2,128)(2,1)S(1)} %all-to-all-done), kind=kOutput, calls=%fused_computation.8 | convolution fusion | flops 469999616 | bytes 59097088 | tf_op jit(solution)/shard_map/secf,efd->secd/dot_general | solution.py:116
  87.6 0.0 all-reduce.2.cloned.1.call-update
  87.7 52.6 %all-reduce.2.cloned.1.call-done = bf16[4,2,2,4096]{3,0,2,1:T(4,128)(2,1)} async-done(((bf16[4,2,2,4096]{3,0,2,1:T(4,128)(2,1)}), bf16[4,2,2,4096]{3,0,2,1:T(4,128)(2,1)}) %all-reduce.2.cloned.1.call-update) | async-done | bytes 131088 | tf_op jit(solution)/shard_map/psum | solution.py:117
  140.3 0.9 convert_convert_fusion
  141.1 0.7 copy.37
  141.8 4.6 %all-to-all-start.1 = ((bf16[4,2,2,2048]{3,2,1,0:T(2,128)(2,1)}), bf16[4,2,2,2048]{3,2,1,0:T(2,128)(2,1)S(1)}, u32[]{:S(2)}, u32[]{:S(2)}) async-start(bf16[4,2,2,2048]{3,2,1,0:T(2,128)(2,1)} %copy.37), calls=%async_computation.1 | async-start | bytes 131072 | tf_op jit(solution)/shard_map/all_to_all | solution.py:120
  146.4 0.1 fusion.48
  146.5 5.7 %all-to-all-done.1 = bf16[4,2,2,2048]{3,2,1,0:T(2,128)(2,1)S(1)} async-done(((bf16[4,2,2,2048]{3,2,1,0:T(2,128)(2,1)}), bf16[4,2,2,2048]{3,2,1,0:T(2,128)(2,1)S(1)}, u32[]{:S(2)}, u32[]{:S(2)}) %all-to-all-start.1) | async-done | bytes 65568 | tf_op jit(solution)/shard_map/all_to_all | solution.py:120
  152.2 0.8 fusion.27
  (11 shorter events, 0.2 us)
Async XLA Ops:
  6.5 3.2 %copy-start = (bf16[4,128,2,128]{3,2,1,0:T(2,128)(2,1)S(1)}, bf16[4,128,2,128]{3,2,1,0:T(2,128)(2,1)}, u32[]{:S(2)}) copy-start(bf16[4,128,2,128]{3,2,1,0:T(2,128)(2,1)} %param.14) | copy-start | bytes 786436
  43.1 11.2 %all-to-all-start = ((bf16[4,2,2,4096]{3,2,1,0:T(2,128)(2,1)}), bf16[4,2,2,4096]{3,2,1,0:T(2,128)(2,1)S(1)}, u32[]{:S(2)}, u32[]{:S(2)}) async-start(bf16[4,2,2,4096]{3,2,1,0:T(2,128)(2,1)} %bitcast.3), calls=%async_computation | async-start | bytes 262144 | tf_op jit(solution)/shard_map/all_to_all | solution.py:112
  48.3 92.0 %all-reduce.2.cloned.1.call-start = ((), (), s32[]{:S(2)}) async-start(), calls=%async_computation.2 | async-start | bytes 262144 | tf_op jit(solution)/shard_map/psum | solution.py:117
  141.8 10.3 %all-to-all-start.1 = ((bf16[4,2,2,2048]{3,2,1,0:T(2,128)(2,1)}), bf16[4,2,2,2048]{3,2,1,0:T(2,128)(2,1)S(1)}, u32[]{:S(2)}, u32[]{:S(2)}) async-start(bf16[4,2,2,2048]{3,2,1,0:T(2,128)(2,1)} %copy.37), calls=%async_computation.1 | async-start | bytes 131072 | tf_op jit(solution)/shard_map/all_to_all | solution.py:120
Sparse Core Ops, SparseCore 0:
  87.8 52.4 all-reduce.1
